TPU v7x, 32 devices: a whole 2x2x4 slice. The times are simulated.
32 devices in a mesh: win: 2 (over core), grp: 16 (over z, y, x).
Axes of the slice: x: 2, y: 2, z: 4, core: 2. Of those that a mesh axis runs over, the one named last changes fastest.
Arguments:
- atom_table: float32 [4, 6, 24576], P('win', None, 'grp'), as said below
- row_blocks: int32 [4, 1024], P('win', 'grp'), may hold values from 0 to 191, as said below
- col_blocks: int32 [4, 1024], P('win', 'grp'), may hold values from 0 to 191, as said below
- lambdas: float32 [4], replicated, may hold values from 0 to 1, as said below
- inverse_temp: float32 [1], replicated, may hold values from 20 to 80
- parity: int32 [1], replicated, may hold values from 0 to 1073741823
- thresholds: int32 [4], replicated, may hold values from 0 to 1073741823
Outputs:
- energies: float32 [4, 3], P('win')
- margins: float32 [4], P('win')
- profile: float32 [4], P('win')
Inputs may be any that keep to these rules, and one draw needn't show every extreme that they name: `row_blocks`: the first block of each pair listed on index g of grp lies in that index's share of atoms: blocks g * 12 to (g + 1) * 12 - 1. `col_blocks`: the list of one index of grp names blocks of any one index of grp (itself included) at most 5 times; in each window some index of grp has exactly 5 of its blocks named in every list of that window. `lambdas`: strictly increasing. `atom_table`: field 4 lies in 0.7 to 1.4 and field 5 in 0.6 to 1.4.
All inputs are finite; a program needn't handle non-finite values.
Results may differ from a plain program's by a relative error of at most 0.0003.
Values sent between devices are 32-bit elements; how exact they have to be, the bound alone decides.
No kernel may reach another device: no remote copies, remote signals or barrier semaphores. Data moves between devices by JAX's collectives and lax.ppermute only.
A program may use at most 64 MiB of HBM per device.

v0:
```python
import jax
import jax.numpy as jnp
from jax import lax
from jax.sharding import PartitionSpec as P

TILE = 128
tiles_per_step = 16


def from_behind(shard, axis, by):
    peers = lax.axis_size(axis)
    pairs = [(i, i + by) for i in range(peers) if 0 <= i + by < peers]
    return lax.ppermute(shard, axis, pairs)


def entering(part, axis, combine, identity):
    place = lax.axis_index(axis)
    gathered = lax.all_gather(part, axis)
    state = jnp.zeros_like(part) + jnp.asarray(identity, part.dtype)

    def one(step, state):
        return combine(state, lax.dynamic_index_in_dim(gathered, step, 0, False))

    return lax.fori_loop(0, place, one, state)


def pair_energy(row_data, col_data, same_block, lambda_set):
    delta_x = row_data[0][:, :, None] - col_data[0][:, None, :]
    delta_y = row_data[1][:, :, None] - col_data[1][:, None, :]
    delta_z = row_data[2][:, :, None] - col_data[2][:, None, :]
    distance = delta_x * delta_x + delta_y * delta_y + delta_z * delta_z
    charge_pair = row_data[3][:, :, None] * col_data[3][:, None, :]
    well_depth = 4.0 * row_data[4][:, :, None] * col_data[4][:, None, :]
    size_pair = row_data[5][:, :, None] * col_data[5][:, None, :]
    scaled = distance / size_pair
    scaled_cube = scaled * scaled * scaled
    width_tile = distance.shape[-1]
    diagonal = (
        lax.broadcasted_iota(jnp.int32, (width_tile, width_tile), 0)
        == lax.broadcasted_iota(jnp.int32, (width_tile, width_tile), 1)
    ).astype(jnp.float32)
    keep_mask = 1.0 - same_block[:, None, None] * diagonal[None]
    totals = []
    for number in range(3):
        lam_now = lambda_set[number]
        softened = 1.0 - 0.5 * lam_now + scaled_cube
        inverse = 1.0 / softened
        dispersion = well_depth * (inverse * inverse - inverse)
        coulomb = charge_pair * lax.rsqrt(distance + 2.0 - lam_now)
        totals.append(lam_now * jnp.sum(keep_mask * (dispersion + coulomb)))
    return jnp.stack(totals)


def evaluate(row_all, col_all, same_all, lambda_set):
    count = same_all.shape[0] // tiles_per_step

    def advance(number, total):
        start = number * tiles_per_step
        row_part = lax.dynamic_slice_in_dim(row_all, start, tiles_per_step, 1)
        col_part = lax.dynamic_slice_in_dim(col_all, start, tiles_per_step, 1)
        same_part = lax.dynamic_slice_in_dim(same_all, start, tiles_per_step, 0)
        return total + pair_energy(row_part, col_part, same_part, lambda_set)

    return lax.fori_loop(0, count, advance, jnp.zeros((3,), jnp.float32))


def add_terms(earlier, later):
    return earlier + later


def take_blocks(source, indices):
    return jnp.take(source, indices, axis=1)


def per_device(atom_table, row_blocks, col_blocks, lambdas, inverse_temp, parity, thresholds):
    windows = lax.axis_size("win") * atom_table.shape[0]
    groups = lax.axis_size("grp")
    window_run = atom_table.shape[0]
    member = lax.axis_index("grp")
    first_window = lax.axis_index("win") * window_run
    fields = atom_table.shape[1]
    blocks_own = atom_table.reshape(window_run, fields, -1, TILE)
    own_count = blocks_own.shape[2]
    listed = row_blocks.shape[1]
    row_data = jax.vmap(take_blocks)(blocks_own, row_blocks - member * own_count)
    slot_count = max(2, 5 * listed // (4 * groups))
    peers = jnp.arange(groups, dtype=jnp.int32)
    slot_ids = jnp.arange(slot_count, dtype=jnp.int32)

    def plan(col_ids):
        owner_ids = col_ids // own_count
        within_ids = col_ids - owner_ids * own_count
        owner_hot = (owner_ids[:, None] == peers[None, :]).astype(jnp.int32)
        earlier_hot = jnp.cumsum(owner_hot, axis=0) - owner_hot
        order_rank = jnp.sum(earlier_hot * owner_hot, axis=1)
        matched = owner_hot[:, :, None] * (
            order_rank[:, None, None] == slot_ids[None, None, :]
        ).astype(jnp.int32)
        requests = jnp.sum(matched * (within_ids + 1)[:, None, None], axis=0) - 1
        return (owner_ids * slot_count + order_rank, requests)

    positions, requests = jax.vmap(plan)(col_blocks)
    incoming = lax.all_to_all(requests, "grp", split_axis=1, concat_axis=1, tiled=True)

    def answer(source, asked):
        picked = jnp.take(source, jnp.maximum(asked, 0), axis=1)
        return jnp.where((asked >= 0)[None, :, :, None], picked, 0.0)

    replies = jax.vmap(answer)(blocks_own, incoming)
    returned = lax.all_to_all(replies, "grp", split_axis=2, concat_axis=2, tiled=True)
    flat_back = returned.reshape(window_run, fields, groups * slot_count, TILE)
    col_data = jax.vmap(take_blocks)(flat_back, positions)
    same_all = (row_blocks == col_blocks).astype(jnp.float32)
    window = first_window + jnp.arange(window_run, dtype=jnp.int32)
    below = jnp.maximum(window - 1, 0)
    above = jnp.minimum(window + 1, windows - 1)
    lambda_sets = jnp.stack([lambdas[below], lambdas[window], lambdas[above]], axis=1)
    partial_sums = lax.map(
        lambda pack: evaluate(pack[0], pack[1], pack[2], pack[3]),
        (row_data, col_data, same_all, lambda_sets),
    )
    scale_count = listed * groups * TILE * TILE
    lower_win = jnp.where(jnp.remainder(window - parity[0], 2) == 0, window, window - 1)
    upper_win = lower_win + 1
    has_partner = (lower_win >= 0) & (upper_win < windows)
    lower_safe = jnp.clip(lower_win, 0, windows - 1)
    summed = lax.psum(partial_sums, "grp")
    energy = summed / scale_count
    d_plus = energy[:, 2] - energy[:, 1]
    d_minus = energy[:, 0] - energy[:, 1]
    minus_above = from_behind(d_minus[0:1], "win", -1)
    plus_below = from_behind(d_plus[window_run - 1 : window_run], "win", 1)
    minus_next = jnp.concatenate([d_minus[1:], minus_above])
    plus_prev = jnp.concatenate([plus_below, d_plus[:-1]])
    change = jnp.where(lower_win == window, d_plus + minus_next, plus_prev + d_minus)
    carried = entering(jnp.sum(d_plus)[None], "win", add_terms, jnp.zeros((1,), jnp.float32))
    profile = carried + (jnp.cumsum(d_plus) - d_plus)
    offset_draw = jnp.remainder(thresholds[lower_safe] + parity[0], 1073741824) + 1
    draw_share = offset_draw.astype(jnp.float32) / 1073741824.0
    margins = jnp.where(has_partner, -jnp.log(draw_share) - inverse_temp[0] * change, 0.0)
    return (energy, margins, profile)


def solution(mesh):
    return jax.shard_map(
        per_device,
        mesh=mesh,
        in_specs=(P("win", None, "grp"), P("win", "grp"), P("win", "grp"), P(), P(), P(), P()),
        out_specs=(P("win", None), P("win"), P("win")),
        check_vma=False,
    )
```

profile of v0, /device:TPU:1, one launch (start us, length us, event | category | flops | bytes accessed | tf_op | source)
XLA Modules:
  0.0 197.2 jit_solution(12268638286886576941)
XLA Ops:
  2.8 7.4 %all-to-all-start = ((s32[2,16,5]{2,0,1:T(2,128)}), s32[2,16,5]{2,0,1:T(2,128)S(1)}, u32[]{:S(2)}, u32[]{:S(2)}) async-start(s32[2,16,5]{2,0,1:T(2,128)} %copy.51), calls=%async_computation | async-start | bytes 32768 | tf_op jit(solution)/shard_map/all_to_all | solution.py:103
  11.7 4.7 %all-to-all-done = s32[2,16,5]{2,0,1:T(2,128)S(1)} async-done(((s32[2,16,5]{2,0,1:T(2,128)}), s32[2,16,5]{2,0,1:T(2,128)S(1)}, u32[]{:S(2)}, u32[]{:S(2)}) %all-to-all-start) | async-done | bytes 672 | tf_op jit(solution)/shard_map/all_to_all | solution.py:103
  20.1 3.6 %all-to-all-start.1 = ((f32[2,6,16,5,128]{4,0,3,1,2:T(2,128)}), f32[2,6,16,5,128]{4,0,3,1,2:T(2,128)S(1)}, u32[]{:S(2)}, u32[]{:S(2)}) async-start(f32[2,6,16,5,128]{4,0,3,1,2:T(2,128)} %copy.58), calls=%async_computation.1 | async-start | bytes 983040 | tf_op jit(solution)/shard_map/all_to_all | solution.py:110
  29.7 4.7 %all-to-all-done.1 = f32[2,6,16,5,128]{4,0,3,1,2:T(2,128)S(1)} async-done(((f32[2,6,16,5,128]{4,0,3,1,2:T(2,128)}), f32[2,6,16,5,128]{4,0,3,1,2:T(2,128)S(1)}, u32[]{:S(2)}, u32[]{:S(2)}) %all-to-all-start.1) | async-done | bytes 491552 | tf_op jit(solution)/shard_map/all_to_all | solution.py:110
  36.0 102.3 %while.37 = (s32[]{:T(128)}, f32[2,3]{1,0:T(2,128)S(1)}, f32[2,6,64,128]{3,2,0,1:T(8,128)S(1)}, f32[2,6,64,128]{3,2,0,1:T(8,128)S(1)}, f32[2,64]{1,0:T(2,128)S(1...) while((s32[]{:T(128)}, f32[2,3]{1,0:T(2,128)S(1)}, ...), condition=%wide.region_9.10_spmd, body=%wide.region_3.0_spmd.sunk | while | flops 16812060 | bytes 1377978 | solution.py:118
  38.7 48.4 %while.39 = (s32[]{:T(128)}, f32[3]{0:T(128)S(1)}, f32[3]{0:T(128)S(1)}, f32[64]{0:T(128)S(1)}, f32[6,64,128]{2,1,0:T(8,128)S(1)}, /*index=5*/f32[6,64,128]{2,1,...) while((s32[]{:T(128)}, f32[3]{0:T(128)S(1)}, ...), condition=%wide.region_8.8_spmd.clone, body=%wide.region_4.7_spmd.clone.sunk | while | flops 16812052 | bytes 590521 | solution.py:64
  39.5 4.1 %fusion.50 = (f32[]{:T(128)}, f32[]{:T(128)}) fusion(f32[]{:T(128)} %bitcast.119, f32[16,128]{1,0:T(8,128)S(1)} %get-tuple-element.546, f32[16,128]{1,0:T(8,128)S(1)} %get-tuple-element.547, f32[16,128]{1,0:T(8,128)S(1)} %get-tuple-element.548, f32[16,128]{1,0:T(8,128)S(1)} %get-tuple-element.549, f32[16,128]{1,0:T(8,128)S(1)} %get-tuple-element.550, ...), kind=kLoop, calls=%fused_computation.20.clone.1 | loop fusion | flops 9699326 | bytes 163928 | tf_op jit(solution)/shard_map/while/body/eval_jaxpr/while/body/eval_jaxpr/reduce_sum | solution.py:50
  44.8 3.4 %fusion.51 = f32[]{:T(128)} fusion(f32[]{:T(128)} %bitcast.121, f32[]{:T(128)} %get-tuple-element.604, f32[16,128]{1,0:T(8,128)S(1)} %get-tuple-element.546, f32[16,128]{1,0:T(8,128)S(1)} %get-tuple-element.547, f32[16,128]{1,0:T(8,128)S(1)} %get-tuple-element.548, f32[16,128]{1,0:T(8,128)S(1)} %get-tuple-element.549, ...), kind=kLoop, calls=%fused_computation.23.clone.1 | loop fusion | flops 7077887 | bytes 163916 | tf_op jit(solution)/shard_map/while/body/eval_jaxpr/while/body/eval_jaxpr/reduce_sum | solution.py:50
  51.6 4.1 %fusion.50 = (f32[]{:T(128)}, f32[]{:T(128)}) fusion(f32[]{:T(128)} %bitcast.119, f32[16,128]{1,0:T(8,128)S(1)} %get-tuple-element.546, f32[16,128]{1,0:T(8,128)S(1)} %get-tuple-element.547, f32[16,128]{1,0:T(8,128)S(1)} %get-tuple-element.548, f32[16,128]{1,0:T(8,128)S(1)} %get-tuple-element.549, f32[16,128]{1,0:T(8,128)S(1)} %get-tuple-element.550, ...), kind=kLoop, calls=%fused_computation.20.clone.1 | loop fusion | flops 9699326 | bytes 163928 | tf_op jit(solution)/shard_map/while/body/eval_jaxpr/while/body/eval_jaxpr/reduce_sum | solution.py:50
  56.9 3.4 %fusion.51 = f32[]{:T(128)} fusion(f32[]{:T(128)} %bitcast.121, f32[]{:T(128)} %get-tuple-element.604, f32[16,128]{1,0:T(8,128)S(1)} %get-tuple-element.546, f32[16,128]{1,0:T(8,128)S(1)} %get-tuple-element.547, f32[16,128]{1,0:T(8,128)S(1)} %get-tuple-element.548, f32[16,128]{1,0:T(8,128)S(1)} %get-tuple-element.549, ...), kind=kLoop, calls=%fused_computation.23.clone.1 | loop fusion | flops 7077887 | bytes 163916 | tf_op jit(solution)/shard_map/while/body/eval_jaxpr/while/body/eval_jaxpr/reduce_sum | solution.py:50
  63.7 4.1 %fusion.50 = (f32[]{:T(128)}, f32[]{:T(128)}) fusion(f32[]{:T(128)} %bitcast.119, f32[16,128]{1,0:T(8,128)S(1)} %get-tuple-element.546, f32[16,128]{1,0:T(8,128)S(1)} %get-tuple-element.547, f32[16,128]{1,0:T(8,128)S(1)} %get-tuple-element.548, f32[16,128]{1,0:T(8,128)S(1)} %get-tuple-element.549, f32[16,128]{1,0:T(8,128)S(1)} %get-tuple-element.550, ...), kind=kLoop, calls=%fused_computation.20.clone.1 | loop fusion | flops 9699326 | bytes 163928 | tf_op jit(solution)/shard_map/while/body/eval_jaxpr/while/body/eval_jaxpr/reduce_sum | solution.py:50
  69.0 3.4 %fusion.51 = f32[]{:T(128)} fusion(f32[]{:T(128)} %bitcast.121, f32[]{:T(128)} %get-tuple-element.604, f32[16,128]{1,0:T(8,128)S(1)} %get-tuple-element.546, f32[16,128]{1,0:T(8,128)S(1)} %get-tuple-element.547, f32[16,128]{1,0:T(8,128)S(1)} %get-tuple-element.548, f32[16,128]{1,0:T(8,128)S(1)} %get-tuple-element.549, ...), kind=kLoop, calls=%fused_computation.23.clone.1 | loop fusion | flops 7077887 | bytes 163916 | tf_op jit(solution)/shard_map/while/body/eval_jaxpr/while/body/eval_jaxpr/reduce_sum | solution.py:50
  75.8 4.1 %fusion.50 = (f32[]{:T(128)}, f32[]{:T(128)}) fusion(f32[]{:T(128)} %bitcast.119, f32[16,128]{1,0:T(8,128)S(1)} %get-tuple-element.546, f32[16,128]{1,0:T(8,128)S(1)} %get-tuple-element.547, f32[16,128]{1,0:T(8,128)S(1)} %get-tuple-element.548, f32[16,128]{1,0:T(8,128)S(1)} %get-tuple-element.549, f32[16,128]{1,0:T(8,128)S(1)} %get-tuple-element.550, ...), kind=kLoop, calls=%fused_computation.20.clone.1 | loop fusion | flops 9699326 | bytes 163928 | tf_op jit(solution)/shard_map/while/body/eval_jaxpr/while/body/eval_jaxpr/reduce_sum | solution.py:50
  81.1 3.4 %fusion.51 = f32[]{:T(128)} fusion(f32[]{:T(128)} %bitcast.121, f32[]{:T(128)} %get-tuple-element.604, f32[16,128]{1,0:T(8,128)S(1)} %get-tuple-element.546, f32[16,128]{1,0:T(8,128)S(1)} %get-tuple-element.547, f32[16,128]{1,0:T(8,128)S(1)} %get-tuple-element.548, f32[16,128]{1,0:T(8,128)S(1)} %get-tuple-element.549, ...), kind=kLoop, calls=%fused_computation.23.clone.1 | loop fusion | flops 7077887 | bytes 163916 | tf_op jit(solution)/shard_map/while/body/eval_jaxpr/while/body/eval_jaxpr/reduce_sum | solution.py:50
  89.8 48.4 %while.39 = (s32[]{:T(128)}, f32[3]{0:T(128)S(1)}, f32[3]{0:T(128)S(1)}, f32[64]{0:T(128)S(1)}, f32[6,64,128]{2,1,0:T(8,128)S(1)}, /*index=5*/f32[6,64,128]{2,1,...) while((s32[]{:T(128)}, f32[3]{0:T(128)S(1)}, ...), condition=%wide.region_8.8_spmd.clone, body=%wide.region_4.7_spmd.clone.sunk | while | flops 16812052 | bytes 590521 | solution.py:64
  90.6 4.1 %fusion.50 = (f32[]{:T(128)}, f32[]{:T(128)}) fusion(f32[]{:T(128)} %bitcast.119, f32[16,128]{1,0:T(8,128)S(1)} %get-tuple-element.546, f32[16,128]{1,0:T(8,128)S(1)} %get-tuple-element.547, f32[16,128]{1,0:T(8,128)S(1)} %get-tuple-element.548, f32[16,128]{1,0:T(8,128)S(1)} %get-tuple-element.549, f32[16,128]{1,0:T(8,128)S(1)} %get-tuple-element.550, ...), kind=kLoop, calls=%fused_computation.20.clone.1 | loop fusion | flops 9699326 | bytes 163928 | tf_op jit(solution)/shard_map/while/body/eval_jaxpr/while/body/eval_jaxpr/reduce_sum | solution.py:50
  96.0 3.4 %fusion.51 = f32[]{:T(128)} fusion(f32[]{:T(128)} %bitcast.121, f32[]{:T(128)} %get-tuple-element.604, f32[16,128]{1,0:T(8,128)S(1)} %get-tuple-element.546, f32[16,128]{1,0:T(8,128)S(1)} %get-tuple-element.547, f32[16,128]{1,0:T(8,128)S(1)} %get-tuple-element.548, f32[16,128]{1,0:T(8,128)S(1)} %get-tuple-element.549, ...), kind=kLoop, calls=%fused_computation.23.clone.1 | loop fusion | flops 7077887 | bytes 163916 | tf_op jit(solution)/shard_map/while/body/eval_jaxpr/while/body/eval_jaxpr/reduce_sum | solution.py:50
  102.7 4.1 %fusion.50 = (f32[]{:T(128)}, f32[]{:T(128)}) fusion(f32[]{:T(128)} %bitcast.119, f32[16,128]{1,0:T(8,128)S(1)} %get-tuple-element.546, f32[16,128]{1,0:T(8,128)S(1)} %get-tuple-element.547, f32[16,128]{1,0:T(8,128)S(1)} %get-tuple-element.548, f32[16,128]{1,0:T(8,128)S(1)} %get-tuple-element.549, f32[16,128]{1,0:T(8,128)S(1)} %get-tuple-element.550, ...), kind=kLoop, calls=%fused_computation.20.clone.1 | loop fusion | flops 9699326 | bytes 163928 | tf_op jit(solution)/shard_map/while/body/eval_jaxpr/while/body/eval_jaxpr/reduce_sum | solution.py:50
  114.8 4.1 %fusion.50 = (f32[]{:T(128)}, f32[]{:T(128)}) fusion(f32[]{:T(128)} %bitcast.119, f32[16,128]{1,0:T(8,128)S(1)} %get-tuple-element.546, f32[16,128]{1,0:T(8,128)S(1)} %get-tuple-element.547, f32[16,128]{1,0:T(8,128)S(1)} %get-tuple-element.548, f32[16,128]{1,0:T(8,128)S(1)} %get-tuple-element.549, f32[16,128]{1,0:T(8,128)S(1)} %get-tuple-element.550, ...), kind=kLoop, calls=%fused_computation.20.clone.1 | loop fusion | flops 9699326 | bytes 163928 | tf_op jit(solution)/shard_map/while/body/eval_jaxpr/while/body/eval_jaxpr/reduce_sum | solution.py:50
  126.9 4.1 %fusion.50 = (f32[]{:T(128)}, f32[]{:T(128)}) fusion(f32[]{:T(128)} %bitcast.119, f32[16,128]{1,0:T(8,128)S(1)} %get-tuple-element.546, f32[16,128]{1,0:T(8,128)S(1)} %get-tuple-element.547, f32[16,128]{1,0:T(8,128)S(1)} %get-tuple-element.548, f32[16,128]{1,0:T(8,128)S(1)} %get-tuple-element.549, f32[16,128]{1,0:T(8,128)S(1)} %get-tuple-element.550, ...), kind=kLoop, calls=%fused_computation.20.clone.1 | loop fusion | flops 9699326 | bytes 163928 | tf_op jit(solution)/shard_map/while/body/eval_jaxpr/while/body/eval_jaxpr/reduce_sum | solution.py:50
  132.2 3.4 %fusion.51 = f32[]{:T(128)} fusion(f32[]{:T(128)} %bitcast.121, f32[]{:T(128)} %get-tuple-element.604, f32[16,128]{1,0:T(8,128)S(1)} %get-tuple-element.546, f32[16,128]{1,0:T(8,128)S(1)} %get-tuple-element.547, f32[16,128]{1,0:T(8,128)S(1)} %get-tuple-element.548, f32[16,128]{1,0:T(8,128)S(1)} %get-tuple-element.549, ...), kind=kLoop, calls=%fused_computation.23.clone.1 | loop fusion | flops 7077887 | bytes 163916 | tf_op jit(solution)/shard_map/while/body/eval_jaxpr/while/body/eval_jaxpr/reduce_sum | solution.py:50
  138.3 34.5 %psum.7 = f32[2,3]{1,0:T(2,128)S(1)} all-reduce(f32[2,3]{1,0:T(2,128)S(1)} %get-tuple-element.224), channel_id=1, replica_groups=mesh['win'=2,'grp'=16] {'grp'}, use_global_device_ids=true, to_apply=%region_10.11 | all-reduce | flops 6 | bytes 48 | tf_op jit(solution)/shard_map/psum | solution.py:127
  174.1 11.6 %collective-permute-start = (f32[1]{0:T(128)}, f32[1]{0:T(128)}, u32[]{:S(2)}, u32[]{:S(2)}) collective-permute-start(f32[1]{0:T(128)} %bitcast.29), channel_id=1, source_target_pairs={{16,0},{17,1},{18,2},{19,3},{20,4},{21,5},{22,6},{23,7},{24,8},{25... | collective-permute-start | bytes 20 | tf_op jit(solution)/shard_map/ppermute | solution.py:13
  188.9 3.8 %all-reduce = f32[2]{0:T(128)S(1)} all-reduce(f32[2]{0:T(128)S(1)} %dynamic-update-slice), channel_id=1, replica_groups=mesh['win'=2,'grp'=16] {'win'}, use_global_device_ids=true, to_apply=%add | all-reduce | flops 2 | bytes 16
  (132 shorter events, 38.2 us)
Async XLA Ops:
  0.6 24.3 %copy-start = (f32[4]{0:T(128)S(1)}, f32[4]{0:T(128)}, u32[]{:S(2)}) copy-start(f32[4]{0:T(128)} %param.16) | copy-start | bytes 52
  1.8 9.8 %copy-start.2 = (f32[2,6,1536]{2,0,1:T(2,128)S(1)}, f32[2,6,1536]{2,0,1:T(2,128)}, u32[]{:S(2)}) copy-start(f32[2,6,1536]{2,0,1:T(2,128)} %param.13) | copy-start | bytes 221188
  2.8 13.6 %all-to-all-start = ((s32[2,16,5]{2,0,1:T(2,128)}), s32[2,16,5]{2,0,1:T(2,128)S(1)}, u32[]{:S(2)}, u32[]{:S(2)}) async-start(s32[2,16,5]{2,0,1:T(2,128)} %copy.51), calls=%async_computation | async-start | bytes 32768 | tf_op jit(solution)/shard_map/all_to_all | solution.py:103
  10.8 0.7 copy-start.5
  20.1 14.3 %all-to-all-start.1 = ((f32[2,6,16,5,128]{4,0,3,1,2:T(2,128)}), f32[2,6,16,5,128]{4,0,3,1,2:T(2,128)S(1)}, u32[]{:S(2)}, u32[]{:S(2)}) async-start(f32[2,6,16,5,128]{4,0,3,1,2:T(2,128)} %copy.58), calls=%async_computation.1 | async-start | bytes 983040 | tf_op jit(solution)/shard_map/all_to_all | solution.py:110
  26.2 2.1 %copy-start.1 = (s32[4]{0:T(128)S(1)}, s32[4]{0:T(128)}, u32[]{:S(2)}) copy-start(s32[4]{0:T(128)} %param.19) | copy-start | bytes 52
  27.0 0.7 copy-start.6
  29.0 0.7 copy-start.4
  172.8 0.7 copy-start.3
  174.1 20.0 %collective-permute-start = (f32[1]{0:T(128)}, f32[1]{0:T(128)}, u32[]{:S(2)}, u32[]{:S(2)}) collective-permute-start(f32[1]{0:T(128)} %bitcast.29), channel_id=1, source_target_pairs={{16,0},{17,1},{18,2},{19,3},{20,4},{21,5},{22,6},{23,7},{24,8},{25... | collective-permute-start | bytes 20 | tf_op jit(solution)/shard_map/ppermute | solution.py:13
  187.6 6.5 %collective-permute-start.1 = (f32[1]{0:T(128)}, f32[1]{0:T(128)}, u32[]{:S(2)}, u32[]{:S(2)}) collective-permute-start(f32[1]{0:T(128)} %bitcast.30), channel_id=1, source_target_pairs={{0,16},{1,17},{2,18},{3,19},{4,20},{5,21},{6,22},{7,23},{8,24},{9,... | collective-permute-start | bytes 20 | tf_op jit(solution)/shard_map/ppermute | solution.py:13
where the time goes:
time: 198 us; the launch traced here: 197 us
  other arithmetic  66.4 us (34%)
  blocking collectives  38.3 us (19%)
  loops' own time  35.2 us (18%)
  starting transfers between devices  23.8 us (12%)
  local copies, waits for them, and re-layouts  22 us (11%)
  waiting for transfers between devices  9.33 us (5%)
  between operations  2.23 us (1%)
    reduce_sum x16, other arithmetic, pair_energy(): totals.append(lam_now * jnp.sum(keep_mask * (dispersion + coulomb)))  59.4 us
    psum x1, blocking collectives, per_device(): summed = lax.psum(partial_sums, 'grp')  34.5 us
    another operation x2, loops' own time, evaluate(): return lax.fori_loop(0, count, advance, jnp.zeros((3,), jnp.float32))  30.6 us
    ppermute x2, starting transfers between devices, from_behind(): return lax.ppermute(shard, axis, pairs)  12.9 us
    all_to_all x1, starting transfers between devices, per_device(): lax.all_to_all(requests, 'grp', split_axis=1, concat_axis=1, tiled=True)  7.4 us
    slice x10, local copies, waits for them, and re-layouts, pair_energy(): lam_now = lambda_set[number]  6.66 us
    all_to_all x1, waiting for transfers between devices, per_device(): lax.all_to_all(replies, 'grp', split_axis=2, concat_axis=2, tiled=True)  4.67 us
    all_to_all x1, waiting for transfers between devices, per_device(): lax.all_to_all(requests, 'grp', split_axis=1, concat_axis=1, tiled=True)  4.66 us
  transfers between devices with their start and end apart: 4, of which 2 were waited for; matrix products, arithmetic and copies ran while one was open for 4% of the time, Pallas kernels for 0%

commit v1 on v0

--- a/solution.py
+++ b/solution.py
@@ -5,6 +5,18 @@
 
 TILE = 128
 tiles_per_step = 16
+
+
+def split_up(x, dim, devices):
+    lengths = x.shape
+    blocks = x.reshape(*lengths[:dim], devices, lengths[dim] // devices, *lengths[dim + 1 :])
+    return jnp.moveaxis(blocks, dim, 0)
+
+
+def in_order(blocks, dim):
+    shape = list(blocks.shape[1:])
+    shape[dim] *= blocks.shape[0]
+    return jnp.moveaxis(blocks, 0, dim).reshape(shape)
 
 
 def from_behind(shard, axis, by):
@@ -100,7 +112,14 @@
         return (owner_ids * slot_count + order_rank, requests)
 
     positions, requests = jax.vmap(plan)(col_blocks)
-    incoming = lax.all_to_all(requests, "grp", split_axis=1, concat_axis=1, tiled=True)
+    devices, here = (lax.axis_size("grp"), lax.axis_index("grp"))
+    pieces = split_up(requests, 1, devices)
+    outs = [pieces[here]]
+    for hop in range(1, devices):
+        sent = pieces[here ^ hop]
+        outs.append(lax.ppermute(sent, "grp", [(i_2, i_2 ^ hop) for i_2 in range(devices)]))
+    pieces = jnp.stack(outs)[here ^ jnp.arange(devices)]
+    incoming = in_order(pieces, 1)
 
     def answer(source, asked):
         picked = jnp.take(source, jnp.maximum(asked, 0), axis=1)

time: 198 us -> 218 us (1.10)
  starting transfers between devices: 23.8 us -> 45.3 us
  blocking collectives: 38.3 us -> 35.6 us
    ppermute x0 -> x15, starting transfers between devices: none -> 23.9 us  [per_device(): lax.ppermute(sent, 'grp', [(i_2, i_2 ^ hop) for i_2 in range(devices)])]
    all_to_all x1 -> x0, starting transfers between devices: 7.4 us -> none  [per_device(): lax.all_to_all(requests, 'grp', split_axis=1, concat_axis=1, tiled=True)]
    ppermute x0 -> x15, waiting for transfers between devices: none -> 5.48 us  [per_device(): lax.ppermute(sent, 'grp', [(i_2, i_2 ^ hop) for i_2 in range(devices)])]
    ppermute x2, starting transfers between devices: 12.9 us -> 17.8 us  [from_behind(): return lax.ppermute(shard, axis, pairs)]
    all_to_all x1 -> x0, waiting for transfers between devices: 4.66 us -> none  [per_device(): lax.all_to_all(requests, 'grp', split_axis=1, concat_axis=1, tiled=True)]
    psum x1, blocking collectives: 34.5 us -> 31.8 us  [per_device(): summed = lax.psum(partial_sums, 'grp')]
  transfers between devices with their start and end apart: 4 -> 18, of which waited for: 2 -> 3; matrix products, arithmetic and copies ran while one was open for 4% -> 4% of each run, Pallas kernels for 0% -> 0%
where the time goes in v1:
time: 218 us; the launch traced here: 217 us
  other arithmetic  67.3 us (31%)
  starting transfers between devices  45.3 us (21%)
  blocking collectives  35.6 us (16%)
  loops' own time  35.1 us (16%)
  local copies, waits for them, and re-layouts  21.9 us (10%)
  waiting for transfers between devices  9.44 us (4%)
  between operations  2.66 us (1%)
    reduce_sum x16, other arithmetic, pair_energy(): totals.append(lam_now * jnp.sum(keep_mask * (dispersion + coulomb)))  59.4 us
    psum x1, blocking collectives, per_device(): summed = lax.psum(partial_sums, 'grp')  31.8 us
    another operation x2, loops' own time, evaluate(): return lax.fori_loop(0, count, advance, jnp.zeros((3,), jnp.float32))  30.6 us
    ppermute x15, starting transfers between devices, per_device(): lax.ppermute(sent, 'grp', [(i_2, i_2 ^ hop) for i_2 in range(devices)])  23.9 us
    ppermute x2, starting transfers between devices, from_behind(): return lax.ppermute(shard, axis, pairs)  17.8 us
    slice x10, local copies, waits for them, and re-layouts, pair_energy(): lam_now = lambda_set[number]  6.66 us
    ppermute x15, waiting for transfers between devices, per_device(): lax.ppermute(sent, 'grp', [(i_2, i_2 ^ hop) for i_2 in range(devices)])  5.48 us
  transfers between devices with their start and end apart: 18, of which 3 were waited for; matrix products, arithmetic and copies ran while one was open for 4% of the time, Pallas kernels for 0%

profile of v1, /device:TPU:1, one launch (start us, length us, event | category | flops | bytes accessed | tf_op | source)
XLA Modules:
  0.0 217.3 jit_solution(13309397440371328471)
XLA Ops:
  24.6 4.3 %collective-permute-start.13 = (s32[2,1,5]{1,2,0:T(8,128)S(1)}, s32[2,1,5]{1,2,0:T(8,128)S(1)}, u32[]{:S(2)}, u32[]{:S(2)}) collective-permute-start(s32[2,1,5]{1,2,0:T(8,128)S(1)} %get-tuple-element.368), channel_id=1, source_target_pairs={{0,14},{1,15},{2,12},{3,13},{4,10},{5,11},{6,8},{7,9},{8,6},{9,7},... | collective-permute-start | bytes 128 | tf_op jit(solution)/shard_map/ppermute | solution.py:120
  30.1 5.1 %collective-permute-done.14 = s32[2,1,5]{1,2,0:T(8,128)S(1)} collective-permute-done((s32[2,1,5]{1,2,0:T(8,128)S(1)}, s32[2,1,5]{1,2,0:T(8,128)S(1)}, u32[]{:S(2)}, u32[]{:S(2)}) %collective-permute-start.14) | collective-permute-done | bytes 72 | tf_op jit(solution)/shard_map/ppermute | solution.py:120
  39.3 3.6 %all-to-all-start = ((f32[2,6,16,5,128]{4,0,3,1,2:T(2,128)}), f32[2,6,16,5,128]{4,0,3,1,2:T(2,128)S(1)}, u32[]{:S(2)}, u32[]{:S(2)}) async-start(f32[2,6,16,5,128]{4,0,3,1,2:T(2,128)} %copy.137), calls=%async_computation | async-start | bytes 983040 | tf_op jit(solution)/shard_map/all_to_all | solution.py:129
  48.2 4.0 %all-to-all-done = f32[2,6,16,5,128]{4,0,3,1,2:T(2,128)S(1)} async-done(((f32[2,6,16,5,128]{4,0,3,1,2:T(2,128)}), f32[2,6,16,5,128]{4,0,3,1,2:T(2,128)S(1)}, u32[]{:S(2)}, u32[]{:S(2)}) %all-to-all-start) | async-done | bytes 491552 | tf_op jit(solution)/shard_map/all_to_all | solution.py:129
  53.8 102.3 %while.37 = (s32[]{:T(128)}, f32[2,3]{1,0:T(2,128)S(1)}, f32[2,6,64,128]{3,2,0,1:T(8,128)S(1)}, f32[2,6,64,128]{3,2,0,1:T(8,128)S(1)}, f32[2,64]{1,0:T(2,128)S(1...) while((s32[]{:T(128)}, f32[2,3]{1,0:T(2,128)S(1)}, ...), condition=%wide.region_9.10_spmd, body=%wide.region_3.0_spmd.sunk | while | flops 16812060 | bytes 1377978 | solution.py:137
  56.5 48.4 %while.39 = (s32[]{:T(128)}, f32[3]{0:T(128)S(1)}, f32[3]{0:T(128)S(1)}, f32[64]{0:T(128)S(1)}, f32[6,64,128]{2,1,0:T(8,128)S(1)}, /*index=5*/f32[6,64,128]{2,1,...) while((s32[]{:T(128)}, f32[3]{0:T(128)S(1)}, ...), condition=%wide.region_8.8_spmd.clone, body=%wide.region_4.7_spmd.clone.sunk | while | flops 16812052 | bytes 590521 | solution.py:76
  57.3 4.1 %fusion.51 = (f32[]{:T(128)}, f32[]{:T(128)}) fusion(f32[]{:T(128)} %bitcast.202, f32[16,128]{1,0:T(8,128)S(1)} %get-tuple-element.568, f32[16,128]{1,0:T(8,128)S(1)} %get-tuple-element.569, f32[16,128]{1,0:T(8,128)S(1)} %get-tuple-element.570, f32[16,128]{1,0:T(8,128)S(1)} %get-tuple-element.571, f32[16,128]{1,0:T(8,128)S(1)} %get-tuple-element.572, ...), kind=kLoop, calls=%fused_computation.21.clone.1 | loop fusion | flops 9699326 | bytes 163928 | tf_op jit(solution)/shard_map/while/body/eval_jaxpr/while/body/eval_jaxpr/reduce_sum | solution.py:62
  62.6 3.4 %fusion.52 = f32[]{:T(128)} fusion(f32[]{:T(128)} %bitcast.204, f32[]{:T(128)} %get-tuple-element.626, f32[16,128]{1,0:T(8,128)S(1)} %get-tuple-element.568, f32[16,128]{1,0:T(8,128)S(1)} %get-tuple-element.569, f32[16,128]{1,0:T(8,128)S(1)} %get-tuple-element.570, f32[16,128]{1,0:T(8,128)S(1)} %get-tuple-element.571, ...), kind=kLoop, calls=%fused_computation.24.clone.1 | loop fusion | flops 7077887 | bytes 163916 | tf_op jit(solution)/shard_map/while/body/eval_jaxpr/while/body/eval_jaxpr/reduce_sum | solution.py:62
  69.4 4.1 %fusion.51 = (f32[]{:T(128)}, f32[]{:T(128)}) fusion(f32[]{:T(128)} %bitcast.202, f32[16,128]{1,0:T(8,128)S(1)} %get-tuple-element.568, f32[16,128]{1,0:T(8,128)S(1)} %get-tuple-element.569, f32[16,128]{1,0:T(8,128)S(1)} %get-tuple-element.570, f32[16,128]{1,0:T(8,128)S(1)} %get-tuple-element.571, f32[16,128]{1,0:T(8,128)S(1)} %get-tuple-element.572, ...), kind=kLoop, calls=%fused_computation.21.clone.1 | loop fusion | flops 9699326 | bytes 163928 | tf_op jit(solution)/shard_map/while/body/eval_jaxpr/while/body/eval_jaxpr/reduce_sum | solution.py:62
  74.7 3.4 %fusion.52 = f32[]{:T(128)} fusion(f32[]{:T(128)} %bitcast.204, f32[]{:T(128)} %get-tuple-element.626, f32[16,128]{1,0:T(8,128)S(1)} %get-tuple-element.568, f32[16,128]{1,0:T(8,128)S(1)} %get-tuple-element.569, f32[16,128]{1,0:T(8,128)S(1)} %get-tuple-element.570, f32[16,128]{1,0:T(8,128)S(1)} %get-tuple-element.571, ...), kind=kLoop, calls=%fused_computation.24.clone.1 | loop fusion | flops 7077887 | bytes 163916 | tf_op jit(solution)/shard_map/while/body/eval_jaxpr/while/body/eval_jaxpr/reduce_sum | solution.py:62
  81.5 4.1 %fusion.51 = (f32[]{:T(128)}, f32[]{:T(128)}) fusion(f32[]{:T(128)} %bitcast.202, f32[16,128]{1,0:T(8,128)S(1)} %get-tuple-element.568, f32[16,128]{1,0:T(8,128)S(1)} %get-tuple-element.569, f32[16,128]{1,0:T(8,128)S(1)} %get-tuple-element.570, f32[16,128]{1,0:T(8,128)S(1)} %get-tuple-element.571, f32[16,128]{1,0:T(8,128)S(1)} %get-tuple-element.572, ...), kind=kLoop, calls=%fused_computation.21.clone.1 | loop fusion | flops 9699326 | bytes 163928 | tf_op jit(solution)/shard_map/while/body/eval_jaxpr/while/body/eval_jaxpr/reduce_sum | solution.py:62
  86.8 3.4 %fusion.52 = f32[]{:T(128)} fusion(f32[]{:T(128)} %bitcast.204, f32[]{:T(128)} %get-tuple-element.626, f32[16,128]{1,0:T(8,128)S(1)} %get-tuple-element.568, f32[16,128]{1,0:T(8,128)S(1)} %get-tuple-element.569, f32[16,128]{1,0:T(8,128)S(1)} %get-tuple-element.570, f32[16,128]{1,0:T(8,128)S(1)} %get-tuple-element.571, ...), kind=kLoop, calls=%fused_computation.24.clone.1 | loop fusion | flops 7077887 | bytes 163916 | tf_op jit(solution)/shard_map/while/body/eval_jaxpr/while/body/eval_jaxpr/reduce_sum | solution.py:62
  93.6 4.1 %fusion.51 = (f32[]{:T(128)}, f32[]{:T(128)}) fusion(f32[]{:T(128)} %bitcast.202, f32[16,128]{1,0:T(8,128)S(1)} %get-tuple-element.568, f32[16,128]{1,0:T(8,128)S(1)} %get-tuple-element.569, f32[16,128]{1,0:T(8,128)S(1)} %get-tuple-element.570, f32[16,128]{1,0:T(8,128)S(1)} %get-tuple-element.571, f32[16,128]{1,0:T(8,128)S(1)} %get-tuple-element.572, ...), kind=kLoop, calls=%fused_computation.21.clone.1 | loop fusion | flops 9699326 | bytes 163928 | tf_op jit(solution)/shard_map/while/body/eval_jaxpr/while/body/eval_jaxpr/reduce_sum | solution.py:62
  98.9 3.4 %fusion.52 = f32[]{:T(128)} fusion(f32[]{:T(128)} %bitcast.204, f32[]{:T(128)} %get-tuple-element.626, f32[16,128]{1,0:T(8,128)S(1)} %get-tuple-element.568, f32[16,128]{1,0:T(8,128)S(1)} %get-tuple-element.569, f32[16,128]{1,0:T(8,128)S(1)} %get-tuple-element.570, f32[16,128]{1,0:T(8,128)S(1)} %get-tuple-element.571, ...), kind=kLoop, calls=%fused_computation.24.clone.1 | loop fusion | flops 7077887 | bytes 163916 | tf_op jit(solution)/shard_map/while/body/eval_jaxpr/while/body/eval_jaxpr/reduce_sum | solution.py:62
  107.7 48.4 %while.39 = (s32[]{:T(128)}, f32[3]{0:T(128)S(1)}, f32[3]{0:T(128)S(1)}, f32[64]{0:T(128)S(1)}, f32[6,64,128]{2,1,0:T(8,128)S(1)}, /*index=5*/f32[6,64,128]{2,1,...) while((s32[]{:T(128)}, f32[3]{0:T(128)S(1)}, ...), condition=%wide.region_8.8_spmd.clone, body=%wide.region_4.7_spmd.clone.sunk | while | flops 16812052 | bytes 590521 | solution.py:76
  108.5 4.1 %fusion.51 = (f32[]{:T(128)}, f32[]{:T(128)}) fusion(f32[]{:T(128)} %bitcast.202, f32[16,128]{1,0:T(8,128)S(1)} %get-tuple-element.568, f32[16,128]{1,0:T(8,128)S(1)} %get-tuple-element.569, f32[16,128]{1,0:T(8,128)S(1)} %get-tuple-element.570, f32[16,128]{1,0:T(8,128)S(1)} %get-tuple-element.571, f32[16,128]{1,0:T(8,128)S(1)} %get-tuple-element.572, ...), kind=kLoop, calls=%fused_computation.21.clone.1 | loop fusion | flops 9699326 | bytes 163928 | tf_op jit(solution)/shard_map/while/body/eval_jaxpr/while/body/eval_jaxpr/reduce_sum | solution.py:62
  113.8 3.4 %fusion.52 = f32[]{:T(128)} fusion(f32[]{:T(128)} %bitcast.204, f32[]{:T(128)} %get-tuple-element.626, f32[16,128]{1,0:T(8,128)S(1)} %get-tuple-element.568, f32[16,128]{1,0:T(8,128)S(1)} %get-tuple-element.569, f32[16,128]{1,0:T(8,128)S(1)} %get-tuple-element.570, f32[16,128]{1,0:T(8,128)S(1)} %get-tuple-element.571, ...), kind=kLoop, calls=%fused_computation.24.clone.1 | loop fusion | flops 7077887 | bytes 163916 | tf_op jit(solution)/shard_map/while/body/eval_jaxpr/while/body/eval_jaxpr/reduce_sum | solution.py:62
  120.6 4.1 %fusion.51 = (f32[]{:T(128)}, f32[]{:T(128)}) fusion(f32[]{:T(128)} %bitcast.202, f32[16,128]{1,0:T(8,128)S(1)} %get-tuple-element.568, f32[16,128]{1,0:T(8,128)S(1)} %get-tuple-element.569, f32[16,128]{1,0:T(8,128)S(1)} %get-tuple-element.570, f32[16,128]{1,0:T(8,128)S(1)} %get-tuple-element.571, f32[16,128]{1,0:T(8,128)S(1)} %get-tuple-element.572, ...), kind=kLoop, calls=%fused_computation.21.clone.1 | loop fusion | flops 9699326 | bytes 163928 | tf_op jit(solution)/shard_map/while/body/eval_jaxpr/while/body/eval_jaxpr/reduce_sum | solution.py:62
  125.9 3.4 %fusion.52 = f32[]{:T(128)} fusion(f32[]{:T(128)} %bitcast.204, f32[]{:T(128)} %get-tuple-element.626, f32[16,128]{1,0:T(8,128)S(1)} %get-tuple-element.568, f32[16,128]{1,0:T(8,128)S(1)} %get-tuple-element.569, f32[16,128]{1,0:T(8,128)S(1)} %get-tuple-element.570, f32[16,128]{1,0:T(8,128)S(1)} %get-tuple-element.571, ...), kind=kLoop, calls=%fused_computation.24.clone.1 | loop fusion | flops 7077887 | bytes 163916 | tf_op jit(solution)/shard_map/while/body/eval_jaxpr/while/body/eval_jaxpr/reduce_sum | solution.py:62
  132.7 4.1 %fusion.51 = (f32[]{:T(128)}, f32[]{:T(128)}) fusion(f32[]{:T(128)} %bitcast.202, f32[16,128]{1,0:T(8,128)S(1)} %get-tuple-element.568, f32[16,128]{1,0:T(8,128)S(1)} %get-tuple-element.569, f32[16,128]{1,0:T(8,128)S(1)} %get-tuple-element.570, f32[16,128]{1,0:T(8,128)S(1)} %get-tuple-element.571, f32[16,128]{1,0:T(8,128)S(1)} %get-tuple-element.572, ...), kind=kLoop, calls=%fused_computation.21.clone.1 | loop fusion | flops 9699326 | bytes 163928 | tf_op jit(solution)/shard_map/while/body/eval_jaxpr/while/body/eval_jaxpr/reduce_sum | solution.py:62
  144.8 4.1 %fusion.51 = (f32[]{:T(128)}, f32[]{:T(128)}) fusion(f32[]{:T(128)} %bitcast.202, f32[16,128]{1,0:T(8,128)S(1)} %get-tuple-element.568, f32[16,128]{1,0:T(8,128)S(1)} %get-tuple-element.569, f32[16,128]{1,0:T(8,128)S(1)} %get-tuple-element.570, f32[16,128]{1,0:T(8,128)S(1)} %get-tuple-element.571, f32[16,128]{1,0:T(8,128)S(1)} %get-tuple-element.572, ...), kind=kLoop, calls=%fused_computation.21.clone.1 | loop fusion | flops 9699326 | bytes 163928 | tf_op jit(solution)/shard_map/while/body/eval_jaxpr/while/body/eval_jaxpr/reduce_sum | solution.py:62
  156.1 31.8 %psum.7 = f32[2,3]{1,0:T(2,128)S(1)} all-reduce(f32[2,3]{1,0:T(2,128)S(1)} %get-tuple-element.224), channel_id=1, replica_groups=mesh['win'=2,'grp'=16] {'grp'}, use_global_device_ids=true, to_apply=%region_10.11 | all-reduce | flops 6 | bytes 48 | tf_op jit(solution)/shard_map/psum | solution.py:146
  189.2 16.5 %collective-permute-start.15 = (f32[1]{0:T(128)}, f32[1]{0:T(128)}, u32[]{:S(2)}, u32[]{:S(2)}) collective-permute-start(f32[1]{0:T(128)} %bitcast.55), channel_id=1, source_target_pairs={{16,0},{17,1},{18,2},{19,3},{20,4},{21,5},{22,6},{23,7},{24,8},{25... | collective-permute-start | bytes 20 | tf_op jit(solution)/shard_map/ppermute | solution.py:25
  209.0 3.8 %all-reduce = f32[2]{0:T(128)S(1)} all-reduce(f32[2]{0:T(128)S(1)} %dynamic-update-slice), channel_id=1, replica_groups=mesh['win'=2,'grp'=16] {'win'}, use_global_device_ids=true, to_apply=%add | all-reduce | flops 2 | bytes 16
  (193 shorter events, 59.0 us)
Async XLA Ops:
  0.6 43.5 %copy-start = (f32[4]{0:T(128)S(1)}, f32[4]{0:T(128)}, u32[]{:S(2)}) copy-start(f32[4]{0:T(128)} %param.16) | copy-start | bytes 52
  0.7 0.7 copy-start.4
  2.2 6.2 %copy-start.2 = (f32[2,6,1536]{2,0,1:T(2,128)S(1)}, f32[2,6,1536]{2,0,1:T(2,128)}, u32[]{:S(2)}) copy-start(f32[2,6,1536]{2,0,1:T(2,128)} %param.13) | copy-start | bytes 221188
  2.5 7.5 %collective-permute-start = (s32[2,1,5]{1,2,0:T(8,128)S(1)}, s32[2,1,5]{1,2,0:T(8,128)S(1)}, u32[]{:S(2)}, u32[]{:S(2)}) collective-permute-start(s32[2,1,5]{1,2,0:T(8,128)S(1)} %get-tuple-element.381), channel_id=1, source_target_pairs={{0,1},{1,0},{2,3},{3,2},{4,5},{5,4},{6,7},{7,6},{8,9},{9,8},{10,11... | collective-permute-start | bytes 128 | tf_op jit(solution)/shard_map/ppermute | solution.py:120
  4.5 7.8 %collective-permute-start.1 = (s32[2,1,5]{1,2,0:T(8,128)S(1)}, s32[2,1,5]{1,2,0:T(8,128)S(1)}, u32[]{:S(2)}, u32[]{:S(2)}) collective-permute-start(s32[2,1,5]{1,2,0:T(8,128)S(1)} %get-tuple-element.380), channel_id=1, source_target_pairs={{0,2},{1,3},{2,0},{3,1},{4,6},{5,7},{6,4},{7,5},{8,10},{9,11},{10,... | collective-permute-start | bytes 128 | tf_op jit(solution)/shard_map/ppermute | solution.py:120
  5.8 6.8 %collective-permute-start.2 = (s32[2,1,5]{1,2,0:T(8,128)S(1)}, s32[2,1,5]{1,2,0:T(8,128)S(1)}, u32[]{:S(2)}, u32[]{:S(2)}) collective-permute-start(s32[2,1,5]{1,2,0:T(8,128)S(1)} %get-tuple-element.379), channel_id=1, source_target_pairs={{0,3},{1,2},{2,1},{3,0},{4,7},{5,6},{6,5},{7,4},{8,11},{9,10},{10,... | collective-permute-start | bytes 128 | tf_op jit(solution)/shard_map/ppermute | solution.py:120
  5.8 9.3 %collective-permute-start.3 = (s32[2,1,5]{1,2,0:T(8,128)S(1)}, s32[2,1,5]{1,2,0:T(8,128)S(1)}, u32[]{:S(2)}, u32[]{:S(2)}) collective-permute-start(s32[2,1,5]{1,2,0:T(8,128)S(1)} %get-tuple-element.378), channel_id=1, source_target_pairs={{0,4},{1,5},{2,6},{3,7},{4,0},{5,1},{6,2},{7,3},{8,12},{9,13},{10,... | collective-permute-start | bytes 128 | tf_op jit(solution)/shard_map/ppermute | solution.py:120
  7.3 9.1 %collective-permute-start.4 = (s32[2,1,5]{1,2,0:T(8,128)S(1)}, s32[2,1,5]{1,2,0:T(8,128)S(1)}, u32[]{:S(2)}, u32[]{:S(2)}) collective-permute-start(s32[2,1,5]{1,2,0:T(8,128)S(1)} %get-tuple-element.377), channel_id=1, source_target_pairs={{0,5},{1,4},{2,7},{3,6},{4,1},{5,0},{6,3},{7,2},{8,13},{9,12},{10,... | collective-permute-start | bytes 128 | tf_op jit(solution)/shard_map/ppermute | solution.py:120
  9.2 0.7 copy-start.5
  9.9 9.9 %collective-permute-start.5 = (s32[2,1,5]{1,2,0:T(8,128)S(1)}, s32[2,1,5]{1,2,0:T(8,128)S(1)}, u32[]{:S(2)}, u32[]{:S(2)}) collective-permute-start(s32[2,1,5]{1,2,0:T(8,128)S(1)} %get-tuple-element.376), channel_id=1, source_target_pairs={{0,6},{1,7},{2,4},{3,5},{4,2},{5,3},{6,0},{7,1},{8,14},{9,15},{10,... | collective-permute-start | bytes 128 | tf_op jit(solution)/shard_map/ppermute | solution.py:120
  12.4 7.6 %collective-permute-start.6 = (s32[2,1,5]{1,2,0:T(8,128)S(1)}, s32[2,1,5]{1,2,0:T(8,128)S(1)}, u32[]{:S(2)}, u32[]{:S(2)}) collective-permute-start(s32[2,1,5]{1,2,0:T(8,128)S(1)} %get-tuple-element.375), channel_id=1, source_target_pairs={{0,7},{1,6},{2,5},{3,4},{4,3},{5,2},{6,1},{7,0},{8,15},{9,14},{10,... | collective-permute-start | bytes 128 | tf_op jit(solution)/shard_map/ppermute | solution.py:120
  12.6 10.9 %collective-permute-start.7 = (s32[2,1,5]{1,2,0:T(8,128)S(1)}, s32[2,1,5]{1,2,0:T(8,128)S(1)}, u32[]{:S(2)}, u32[]{:S(2)}) collective-permute-start(s32[2,1,5]{1,2,0:T(8,128)S(1)} %get-tuple-element.374), channel_id=1, source_target_pairs={{0,8},{1,9},{2,10},{3,11},{4,12},{5,13},{6,14},{7,15},{8,0},{9,1},... | collective-permute-start | bytes 128 | tf_op jit(solution)/shard_map/ppermute | solution.py:120
  15.2 9.5 %collective-permute-start.8 = (s32[2,1,5]{1,2,0:T(8,128)S(1)}, s32[2,1,5]{1,2,0:T(8,128)S(1)}, u32[]{:S(2)}, u32[]{:S(2)}) collective-permute-start(s32[2,1,5]{1,2,0:T(8,128)S(1)} %get-tuple-element.373), channel_id=1, source_target_pairs={{0,9},{1,8},{2,11},{3,10},{4,13},{5,12},{6,15},{7,14},{8,1},{9,0},... | collective-permute-start | bytes 128 | tf_op jit(solution)/shard_map/ppermute | solution.py:120
  16.3 12.7 %collective-permute-start.9 = (s32[2,1,5]{1,2,0:T(8,128)S(1)}, s32[2,1,5]{1,2,0:T(8,128)S(1)}, u32[]{:S(2)}, u32[]{:S(2)}) collective-permute-start(s32[2,1,5]{1,2,0:T(8,128)S(1)} %get-tuple-element.372), channel_id=1, source_target_pairs={{0,10},{1,11},{2,8},{3,9},{4,14},{5,15},{6,12},{7,13},{8,2},{9,3},... | collective-permute-start | bytes 128 | tf_op jit(solution)/shard_map/ppermute | solution.py:120
  19.8 9.4 %collective-permute-start.10 = (s32[2,1,5]{1,2,0:T(8,128)S(1)}, s32[2,1,5]{1,2,0:T(8,128)S(1)}, u32[]{:S(2)}, u32[]{:S(2)}) collective-permute-start(s32[2,1,5]{1,2,0:T(8,128)S(1)} %get-tuple-element.371), channel_id=1, source_target_pairs={{0,11},{1,10},{2,9},{3,8},{4,15},{5,14},{6,13},{7,12},{8,3},{9,2},... | collective-permute-start | bytes 128 | tf_op jit(solution)/shard_map/ppermute | solution.py:120
  20.0 9.3 %collective-permute-start.11 = (s32[2,1,5]{1,2,0:T(8,128)S(1)}, s32[2,1,5]{1,2,0:T(8,128)S(1)}, u32[]{:S(2)}, u32[]{:S(2)}) collective-permute-start(s32[2,1,5]{1,2,0:T(8,128)S(1)} %get-tuple-element.370), channel_id=1, source_target_pairs={{0,12},{1,13},{2,14},{3,15},{4,8},{5,9},{6,10},{7,11},{8,4},{9,5},... | collective-permute-start | bytes 128 | tf_op jit(solution)/shard_map/ppermute | solution.py:120
  23.5 6.0 %collective-permute-start.12 = (s32[2,1,5]{1,2,0:T(8,128)S(1)}, s32[2,1,5]{1,2,0:T(8,128)S(1)}, u32[]{:S(2)}, u32[]{:S(2)}) collective-permute-start(s32[2,1,5]{1,2,0:T(8,128)S(1)} %get-tuple-element.369), channel_id=1, source_target_pairs={{0,13},{1,12},{2,15},{3,14},{4,9},{5,8},{6,11},{7,10},{8,5},{9,4},... | collective-permute-start | bytes 128 | tf_op jit(solution)/shard_map/ppermute | solution.py:120
  24.6 5.3 %collective-permute-start.13 = (s32[2,1,5]{1,2,0:T(8,128)S(1)}, s32[2,1,5]{1,2,0:T(8,128)S(1)}, u32[]{:S(2)}, u32[]{:S(2)}) collective-permute-start(s32[2,1,5]{1,2,0:T(8,128)S(1)} %get-tuple-element.368), channel_id=1, source_target_pairs={{0,14},{1,15},{2,12},{3,13},{4,10},{5,11},{6,8},{7,9},{8,6},{9,7},... | collective-permute-start | bytes 128 | tf_op jit(solution)/shard_map/ppermute | solution.py:120
  29.0 6.2 %collective-permute-start.14 = (s32[2,1,5]{1,2,0:T(8,128)S(1)}, s32[2,1,5]{1,2,0:T(8,128)S(1)}, u32[]{:S(2)}, u32[]{:S(2)}) collective-permute-start(s32[2,1,5]{1,2,0:T(8,128)S(1)} %get-tuple-element.367), channel_id=1, source_target_pairs={{0,15},{1,14},{2,13},{3,12},{4,11},{5,10},{6,9},{7,8},{8,7},{9,6},... | collective-permute-start | bytes 128 | tf_op jit(solution)/shard_map/ppermute | solution.py:120
  39.3 12.9 %all-to-all-start = ((f32[2,6,16,5,128]{4,0,3,1,2:T(2,128)}), f32[2,6,16,5,128]{4,0,3,1,2:T(2,128)S(1)}, u32[]{:S(2)}, u32[]{:S(2)}) async-start(f32[2,6,16,5,128]{4,0,3,1,2:T(2,128)} %copy.137), calls=%async_computation | async-start | bytes 983040 | tf_op jit(solution)/shard_map/all_to_all | solution.py:129
  45.5 2.1 copy-start.1
  188.0 0.7 copy-start.3
  189.2 24.9 %collective-permute-start.15 = (f32[1]{0:T(128)}, f32[1]{0:T(128)}, u32[]{:S(2)}, u32[]{:S(2)}) collective-permute-start(f32[1]{0:T(128)} %bitcast.55), channel_id=1, source_target_pairs={{16,0},{17,1},{18,2},{19,3},{20,4},{21,5},{22,6},{23,7},{24,8},{25... | collective-permute-start | bytes 20 | tf_op jit(solution)/shard_map/ppermute | solution.py:25
  207.7 6.5 %collective-permute-start.16 = (f32[1]{0:T(128)}, f32[1]{0:T(128)}, u32[]{:S(2)}, u32[]{:S(2)}) collective-permute-start(f32[1]{0:T(128)} %bitcast.56), channel_id=1, source_target_pairs={{0,16},{1,17},{2,18},{3,19},{4,20},{5,21},{6,22},{7,23},{8,24},{9,... | collective-permute-start | bytes 20 | tf_op jit(solution)/shard_map/ppermute | solution.py:25
  (1 other events, 0.7 us)
